TPU v7x, 32 devices: a whole 2x2x4 slice. The times are simulated.
32 devices in a mesh: owner: 16 (over z, y, x), rows: 2 (over core).
Axes of the slice: x: 2, y: 2, z: 4, core: 2. Of those that a mesh axis runs over, the one named last changes fastest.
Arguments:
- train_down: float32 [64, 1024, 2048], P('owner', None, 'rows'), may hold values from -0.1875 to 0.1875
- router_weight: float32 [2048, 64], P('rows', 'owner'), may hold values from -0.125 to 0.125
- router_gain: float32 [2048], P('rows'), may hold values from 0.25 to 1.75
Outputs:
- ready_down: bfloat16 [64, 2048, 1024], P('owner')
- serve_router: bfloat16 [2048, 64], replicated
All inputs are finite; a program needn't handle non-finite values.
Results may differ from a plain program's by a relative error of at most 0.001.
Values may be sent and summed in bfloat16 or wider, within the bound.
A program may use at most 128 MiB of HBM per device.

v0:
```python
import jax
import jax.numpy as jnp
from jax import lax
from jax.sharding import PartitionSpec as P


def on_device(train_down, router_weight, router_gain):
    narrow_down = train_down.astype(jnp.bfloat16)
    ready_down = lax.all_gather(narrow_down, "rows", axis=2, tiled=True)
    ready_down = jnp.transpose(ready_down, (0, 2, 1))
    part_router = (router_weight * router_gain[:, None]).astype(jnp.bfloat16)
    row_router = lax.all_gather(part_router, "rows", axis=0, tiled=True)
    serve_router = lax.all_gather(row_router, "owner", axis=1, tiled=True)
    return (ready_down, serve_router)


def solution(mesh):
    in_specs = (P("owner", None, "rows"), P("rows", "owner"), P("rows"))
    out_specs = (P("owner", None, None), P())
    return jax.shard_map(
        on_device, mesh=mesh, in_specs=in_specs, out_specs=out_specs, check_vma=False
    )
```

profile of v0, /device:TPU:0, one launch (start us, length us, event | category | flops | bytes accessed | tf_op | source)
XLA Modules:
  0.0 88.0 jit_solution(12130074609468698385)
XLA Ops:
  7.2 0.0 copy-start
  7.2 0.0 copy-start.1
  7.2 0.0 all-gather.3.cloned.1.call-start
  7.2 13.6 %copy.6 = bf16[4,1024,1024]{1,2,0:T(8,128)(2,1)} copy(f32[4,1024,1024]{2,1,0:T(8,128)} %param.3) | data formatting | bytes 25165824 | tf_op args[0]
  20.8 0.0 all-gather.3.cloned.1.call-update
  20.8 0.0 copy-done
  20.8 0.0 copy-done.1
  20.9 2.0 %all_gather.10 = bf16[2048,4]{0,1:T(4,128)(2,1)S(1)} all-gather(bf16[1024,4]{0,1:T(4,128)(2,1)S(1)} %multiply_convert_fusion), channel_id=1, replica_groups=mesh['owner'=16,'rows'=2] {'rows'}, dimensions={0}, use_global_device_ids=true | all-gather | bytes 24576 | tf_op jit(solution)/shard_map/all_gather | solution.py:12
  22.8 43.6 %all-gather = bf16[16,4,2048]{2,1,0:T(4,128)(2,1)S(1)} all-gather(bf16[1,4,2048]{2,1,0:T(4,128)(2,1)S(1)} %bitcast.7), channel_id=1, replica_groups=mesh['owner'=16,'rows'=2] {'owner'}, dimensions={0}, use_global_device_ids=true | all-gather | bytes 278528 | tf_op jit(solution)/shard_map/all_gather | solution.py:13
  66.5 0.8 reshape.6
  67.2 0.0 all-gather.3.cloned.1.call-done
  67.2 13.9 %copy.8 = bf16[4,2048,1024]{2,1,0:T(8,128)(2,1)} copy(bf16[4,2048,1024]{2,1,0:T(8,128)(2,1)} %bitcast.5) | data formatting | bytes 33554432
  (1 shorter events, 0.0 us)
Async XLA Ops:
  7.2 13.7 %copy-start = (f32[1024,4]{0,1:T(4,128)S(1)}, f32[1024,4]{0,1:T(4,128)}, u32[]{:S(2)}) copy-start(f32[1024,4]{0,1:T(4,128)} %param.4) | copy-start | bytes 49156
  7.2 13.7 %copy-start.1 = (f32[1024]{0:T(1024)S(1)}, f32[1024]{0:T(1024)}, u32[]{:S(2)}) copy-start(f32[1024]{0:T(1024)} %param.5) | copy-start | bytes 12292
  7.2 60.0 %all-gather.3.cloned.1.call-start = ((), (), s32[]{:S(2)}) async-start(), calls=%async_computation | async-start | bytes 25165824 | tf_op jit(solution)/shard_map/all_gather | solution.py:9
Sparse Core Ops, SparseCore 0:
  20.9 32.7 all-gather.2
where the time goes:
time: 88.4 us; the launch traced here: 88 us
  blocking collectives  45.6 us (52%)
  local copies, waits for them, and re-layouts  28.2 us (32%)
  between operations  14.1 us (16%)
    all_gather x1, blocking collectives, on_device(): serve_router = lax.all_gather(row_router, 'owner', axis=1, tiled=True)  43.6 us
    unnamed x7, local copies, waits for them, and re-layouts  28.2 us
    all_gather x1, blocking collectives, on_device(): row_router = lax.all_gather(part_router, 'rows', axis=0, tiled=True)  1.97 us
  transfers between devices with their start and end apart: 1, of which 0 were waited for; matrix products, arithmetic and copies ran while one was open for 1% of the time, Pallas kernels for 0%

commit v1 on v0

v1 whole, which is shorter than its diff:
```python
import functools

import jax
import jax.numpy as jnp
from jax import lax
from jax.experimental import pallas as pl
from jax.experimental.pallas import tpu as pltpu
from jax.sharding import PartitionSpec as P

MESH = pl.DeviceIdType.MESH
AHEAD = 6


def exchange_kernel(
    owners, rows, tile,
    down, weight, gain, ready, router,
    landed, load_sem, send_sem, recv_sem,
    row_send, row_recv, own_send, own_recv,
):
    owner, row = lax.axis_index("owner"), lax.axis_index("rows")
    experts, _, width = down.shape
    part = weight.shape[1]
    per = width // tile
    steps = experts * per

    def load(i):
        source = down.at[i // per, :, pl.ds(pl.multiple_of((i % per) * tile, tile), tile)]
        return pltpu.make_async_copy(source, landed.at[i], load_sem.at[i])

    def place(i, r):
        start = pl.multiple_of(r * width + (i % per) * tile, tile)
        return ready.at[i // per, pl.ds(start, tile), :]

    def send(i, j):
        return pltpu.make_async_remote_copy(
            src_ref=place(i, row), dst_ref=place(i, row),
            send_sem=send_sem.at[j - 1, i], recv_sem=recv_sem.at[j - 1, i],
            device_id=(owner, lax.rem(row + j, rows)), device_id_type=MESH,
        )

    def row_place(r):
        return router.at[owner, :, pl.ds(pl.multiple_of(r * part, part), part)]

    def row_copy(j):
        return pltpu.make_async_remote_copy(
            src_ref=row_place(row), dst_ref=row_place(row),
            send_sem=row_send.at[j - 1], recv_sem=row_recv.at[j - 1],
            device_id=(owner, lax.rem(row + j, rows)), device_id_type=MESH,
        )

    def own_copy(j):
        return pltpu.make_async_remote_copy(
            src_ref=router.at[owner], dst_ref=router.at[owner],
            send_sem=own_send.at[j - 1], recv_sem=own_recv.at[j - 1],
            device_id=(lax.rem(owner + j, owners), row), device_id_type=MESH,
        )

    ahead = min(AHEAD, steps)
    for i in range(ahead):
        load(i).start()

    barrier = pltpu.get_barrier_semaphore()
    for j in range(1, rows):
        pl.semaphore_signal(
            barrier, inc=1, device_id=(owner, lax.rem(row + j, rows)), device_id_type=MESH)

    @pl.loop(1, owners)
    def _(j):
        pl.semaphore_signal(
            barrier, inc=1, device_id=(lax.rem(owner + j, owners), row), device_id_type=MESH)

    router[owner, :, pl.ds(pl.multiple_of(row * part, part), part)] = (
        weight[...] * gain[...]).astype(jnp.bfloat16)

    def turn(i):
        load(i).wait()
        start = pl.multiple_of(row * width + (i % per) * tile, tile)
        ready[i // per, pl.ds(start, tile), :] = landed[i].T.astype(jnp.bfloat16)

        @pl.when(i + ahead < steps)
        def _():
            load(i + ahead).start()

    turn(0)
    pl.semaphore_wait(barrier, rows - 1 + owners - 1)
    for j in range(1, rows):
        row_copy(j).start()
        send(0, j).start()

    if steps > 1:
        @pl.loop(1, steps)
        def _(i):
            turn(i)
            for j in range(1, rows):
                send(i, j).start()

    for j in range(1, rows):
        row_copy(j).wait()

    @pl.loop(1, owners)
    def _(j):
        own_copy(j).start()

    @pl.loop(1, owners)
    def _(j):
        own_copy(j).wait()

    @pl.loop(0, steps)
    def _(i):
        for j in range(1, rows):
            send(i, j).wait()


def write_kernel(pieces, ready, out, sems):
    size = ready.shape[0] // pieces

    def copy(i):
        span = pl.ds(i * size, size)
        return pltpu.make_async_copy(ready.at[span], out.at[span], sems.at[i])

    for i in range(pieces):
        copy(i).start()
    for i in range(pieces):
        copy(i).wait()


def on_device(owners, rows, train_down, router_weight, router_gain):
    experts, depth, width = train_down.shape
    part, local = router_weight.shape
    tile = min(256, width)
    steps = experts * (width // tile)
    vmem = pl.BlockSpec(memory_space=pltpu.VMEM)
    anywhere = pl.BlockSpec(memory_space=pl.ANY)
    full = rows * width
    ready, router = pl.pallas_call(
        functools.partial(exchange_kernel, owners, rows, tile),
        out_shape=(
            pltpu.VMEM((experts, full, depth), jnp.bfloat16),
            pltpu.VMEM((owners, local, rows * part), jnp.bfloat16),
        ),
        in_specs=[anywhere, vmem, vmem],
        out_specs=(vmem, vmem),
        scratch_shapes=[
            pltpu.VMEM((steps, depth, tile), jnp.float32),
            pltpu.SemaphoreType.DMA((steps,)),
            pltpu.SemaphoreType.DMA((rows - 1, steps)),
            pltpu.SemaphoreType.DMA((rows - 1, steps)),
            pltpu.SemaphoreType.DMA((rows - 1,)),
            pltpu.SemaphoreType.DMA((rows - 1,)),
            pltpu.SemaphoreType.DMA((owners - 1,)),
            pltpu.SemaphoreType.DMA((owners - 1,)),
        ],
        compiler_params=pltpu.CompilerParams(
            collective_id=0, has_side_effects=True, vmem_limit_bytes=22 * 2**20),
        name="exchange",
    )(train_down, router_weight.T, router_gain.reshape(1, part))
    flat = ready.reshape(experts * full, depth)
    pieces = 8
    out = pl.pallas_call(
        functools.partial(write_kernel, pieces),
        out_shape=jax.ShapeDtypeStruct((experts * full, depth), jnp.bfloat16),
        in_specs=[vmem],
        out_specs=anywhere,
        scratch_shapes=[pltpu.SemaphoreType.DMA((pieces,))],
        compiler_params=pltpu.CompilerParams(vmem_limit_bytes=4 * 2**20),
        name="write",
    )(flat)
    serve = router.reshape(owners * local, rows * part).T
    return out.reshape(experts, full, depth), serve


def solution(mesh):
    owners, rows = mesh.shape["owner"], mesh.shape["rows"]
    return jax.shard_map(
        functools.partial(on_device, owners, rows),
        mesh=mesh,
        in_specs=(P("owner", None, "rows"), P("rows", "owner"), P("rows")),
        out_specs=(P("owner", None, None), P()),
        check_vma=False,
    )
```

time: 88.4 us -> 29.5 us (0.33)
  blocking collectives: 45.6 us -> 0 us
  Pallas kernels: 0 us -> 26.4 us
  local copies, waits for them, and re-layouts: 28.2 us -> 2.16 us
  between operations: 14.1 us -> 0.66 us
    all_gather x2 -> x0, blocking collectives: 45.6 us -> none  [the longest x1 43.6 us: on_device(): serve_router = lax.all_gather(row_router, 'owner', axis=1, tiled=True)]
    unnamed x7 -> x4, local copies, waits for them, and re-layouts: 28.2 us -> 1.4 us
    pallas_call x0 -> x2, Pallas kernels: none -> 26.4 us  [the longest x1 20.5 us: on_device(): pl.pallas_call(functools.partial(exchange_kernel, owners, rows, tile), ou...]
  transfers between devices with their start and end apart: 1 -> 0, of which waited for: 0 -> 0; matrix products, arithmetic and copies ran while one was open for 1% -> 0% of each run, Pallas kernels for 0% -> 0%
where the time goes in v1:
time: 29.5 us; the launch traced here: 29.2 us
  Pallas kernels  26.4 us (89%)
  local copies, waits for them, and re-layouts  2.16 us (7%)
  between operations  0.66 us (2%)
    pallas_call x1, Pallas kernels, on_device(): pl.pallas_call(functools.partial(exchange_kernel, owners, rows, tile), ou...  20.5 us
    pallas_call x1, Pallas kernels, on_device(): pl.pallas_call(functools.partial(write_kernel, pieces), out_shape=jax.Sha...  5.92 us
    unnamed x4, local copies, waits for them, and re-layouts  1.4 us
    reshape x1, local copies, waits for them, and re-layouts, on_device(): serve = router.reshape(owners * local, rows * part).T  0.77 us

profile of v1, /device:TPU:0, one launch (start us, length us, event | category | flops | bytes accessed | tf_op | source)
XLA Modules:
  0.0 29.2 jit_solution(196642606462410794)
XLA Ops:
  0.6 0.0 copy-start
  0.6 0.7 %copy-done = f32[1024,4]{0,1:T(4,128)S(1)} copy-done((f32[1024,4]{0,1:T(4,128)S(1)}, f32[1024,4]{0,1:T(4,128)}, u32[]{:S(2)}) %copy-start) | copy-done | bytes 16408
  1.3 0.0 copy-start.1
  1.4 0.7 %copy-done.1 = f32[1024]{0:T(1024)S(1)} copy-done((f32[1024]{0:T(1024)S(1)}, f32[1024]{0:T(1024)}, u32[]{:S(2)}) %copy-start.1) | copy-done | bytes 4120
  2.0 20.5 %exchange.1 = (bf16[4,2048,1024]{2,1,0:T(8,128)(2,1)S(1)}, bf16[16,4,2048]{2,1,0:T(4,128)(2,1)S(1)}) custom-call(f32[4,1024,1024]{2,1,0:T(8,128)} %down.1, f32[4,1024]{1,0:T(4,128)S(1)} %bitcast.6, f32[1,1024]{1,0:T(1,128)S(1)} %bitcast.7), custom_call_target="tpu_custom_call" | custom-call | tf_op jit(solution)/shard_map/exchange/pallas_call | solution.py:135
  22.5 5.9 %write.1 = bf16[8192,1024]{1,0:T(8,128)(2,1)} custom-call(bf16[8192,1024]{1,0:T(8,128)(2,1)S(1)} %bitcast.5), custom_call_target="tpu_custom_call" | custom-call | tf_op jit(solution)/shard_map/write/pallas_call | solution.py:159
  28.5 0.8 %reshape.19 = bf16[64,2048]{1,0:T(8,128)(2,1)} reshape(bf16[16,4,2048]{2,1,0:T(4,128)(2,1)S(1)} %get-tuple-element.5) | data formatting | bytes 524288 | tf_op jit(solution)/shard_map/reshape | solution.py:168
Async XLA Ops:
  0.6 0.7 %copy-start = (f32[1024,4]{0,1:T(4,128)S(1)}, f32[1024,4]{0,1:T(4,128)}, u32[]{:S(2)}) copy-start(f32[1024,4]{0,1:T(4,128)} %param.4) | copy-start | bytes 49156
  1.3 0.7 %copy-start.1 = (f32[1024]{0:T(1024)S(1)}, f32[1024]{0:T(1024)}, u32[]{:S(2)}) copy-start(f32[1024]{0:T(1024)} %param.5) | copy-start | bytes 12292

commit v2 on v1

v2 whole, which is shorter than its diff:
```python
import functools

import jax
import jax.numpy as jnp
from jax import lax
from jax.experimental import pallas as pl
from jax.experimental.pallas import tpu as pltpu
from jax.sharding import PartitionSpec as P

MESH = pl.DeviceIdType.MESH
AHEAD = 6


def exchange_kernel(
    owners, rows, tile,
    down, weight, gain, ready, router,
    landed, weight_here, gain_here, load_sem, small_sem, send_sem, recv_sem,
    row_send, row_recv, own_send, own_recv, near, go, all_in,
):
    owner, row = lax.axis_index("owner"), lax.axis_index("rows")
    experts, _, width = down.shape
    part = weight.shape[1]
    per = width // tile
    steps = experts * per

    def load(i):
        source = down.at[i // per, :, pl.ds(pl.multiple_of((i % per) * tile, tile), tile)]
        return pltpu.make_async_copy(source, landed.at[i], load_sem.at[i])

    def place(i):
        start = pl.multiple_of(row * width + (i % per) * tile, tile)
        return ready.at[i // per, pl.ds(start, tile), :]

    def send(i, j):
        return pltpu.make_async_remote_copy(
            src_ref=place(i), dst_ref=place(i),
            send_sem=send_sem.at[j - 1, i], recv_sem=recv_sem.at[j - 1, i],
            device_id=(owner, lax.rem(row + j, rows)), device_id_type=MESH,
        )

    def row_copy(j):
        mine = router.at[owner, :, pl.ds(pl.multiple_of(row * part, part), part)]
        return pltpu.make_async_remote_copy(
            src_ref=mine, dst_ref=mine,
            send_sem=row_send.at[j - 1], recv_sem=row_recv.at[j - 1],
            device_id=(owner, lax.rem(row + j, rows)), device_id_type=MESH,
        )

    def own_copy(j):
        return pltpu.make_async_remote_copy(
            src_ref=router.at[owner], dst_ref=router.at[owner],
            send_sem=own_send.at[j - 1], recv_sem=own_recv.at[j - 1],
            device_id=(lax.rem(owner + j, owners), row), device_id_type=MESH,
        )

    def signal(sem, o, r):
        pl.semaphore_signal(sem, inc=1, device_id=(o, r), device_id_type=MESH)

    barrier = pltpu.get_barrier_semaphore()

    @pl.when(row == 0)
    def _():
        for r in range(1, rows):
            signal(barrier, owner, r)

    copies = (
        pltpu.make_async_copy(weight, weight_here, small_sem.at[0]),
        pltpu.make_async_copy(gain, gain_here, small_sem.at[1]),
    )
    for copy in copies:
        copy.start()
    ahead = min(AHEAD, steps)
    for i in range(ahead):
        load(i).start()

    @pl.when(row != 0)
    def _():
        pl.semaphore_wait(barrier, 1)
        signal(near, owner, 0)

    @pl.when(row == 0)
    def _():
        pl.semaphore_wait(near, rows - 1)
        for r in range(1, rows):
            signal(go, owner, r)

        @pl.loop(1, owners)
        def _(j):
            signal(barrier, lax.rem(owner + j, owners), 0)

    for copy in copies:
        copy.wait()
    router[owner, :, pl.ds(pl.multiple_of(row * part, part), part)] = (
        weight_here[...] * gain_here[...]).astype(jnp.bfloat16)

    def turn(i):
        load(i).wait()
        start = pl.multiple_of(row * width + (i % per) * tile, tile)
        ready[i // per, pl.ds(start, tile), :] = landed[i].T.astype(jnp.bfloat16)

        @pl.when(i + ahead < steps)
        def _():
            load(i + ahead).start()

    def turn_and_send(i):
        turn(i)
        for j in range(1, rows):
            send(i, j).start()

    turn(0)

    @pl.when(row != 0)
    def _():
        pl.semaphore_wait(go, 1)

    for j in range(1, rows):
        row_copy(j).start()
        send(0, j).start()

    half = max(1, steps // 2)
    if half > 1:
        pl.loop(1, half)(turn_and_send)

    for j in range(1, rows):
        row_copy(j).wait()

    @pl.when(row == 0)
    def _():
        pl.semaphore_wait(barrier, owners - 1)
        for r in range(1, rows):
            signal(all_in, owner, r)

    @pl.when(row != 0)
    def _():
        pl.semaphore_wait(all_in, 1)

    @pl.loop(1, owners)
    def _(j):
        own_copy(j).start()

    if steps > half:
        pl.loop(half, steps)(turn_and_send)

    @pl.loop(0, steps)
    def _(i):
        for j in range(1, rows):
            send(i, j).wait()

    @pl.loop(1, owners)
    def _(j):
        own_copy(j).wait()


def write_kernel(pieces, ready, router, out, serve, sems):
    size = ready.shape[0] // pieces
    local = router.shape[1]

    def copy(i):
        span = pl.ds(i * size, size)
        return pltpu.make_async_copy(ready.at[span], out.at[span], sems.at[i])

    for i in range(pieces):
        copy(i).start()
    for o in range(router.shape[0]):
        serve[o * local:(o + 1) * local, :] = router[o]
    for i in range(pieces):
        copy(i).wait()


def on_device(owners, rows, train_down, router_weight, router_gain):
    experts, depth, width = train_down.shape
    part, local = router_weight.shape
    tile = min(256, width)
    steps = experts * (width // tile)
    vmem = pl.BlockSpec(memory_space=pltpu.VMEM)
    anywhere = pl.BlockSpec(memory_space=pl.ANY)
    full = rows * width
    ready, router = pl.pallas_call(
        functools.partial(exchange_kernel, owners, rows, tile),
        out_shape=(
            pltpu.VMEM((experts, full, depth), jnp.bfloat16),
            pltpu.VMEM((owners, local, rows * part), jnp.bfloat16),
        ),
        in_specs=[anywhere, anywhere, anywhere],
        out_specs=(vmem, vmem),
        scratch_shapes=[
            pltpu.VMEM((steps, depth, tile), jnp.float32),
            pltpu.VMEM((local, part), jnp.float32),
            pltpu.VMEM((1, part), jnp.float32),
            pltpu.SemaphoreType.DMA((steps,)),
            pltpu.SemaphoreType.DMA((2,)),
            pltpu.SemaphoreType.DMA((rows - 1, steps)),
            pltpu.SemaphoreType.DMA((rows - 1, steps)),
            pltpu.SemaphoreType.DMA((rows - 1,)),
            pltpu.SemaphoreType.DMA((rows - 1,)),
            pltpu.SemaphoreType.DMA((owners - 1,)),
            pltpu.SemaphoreType.DMA((owners - 1,)),
            pltpu.SemaphoreType.REGULAR,
            pltpu.SemaphoreType.REGULAR,
            pltpu.SemaphoreType.REGULAR,
        ],
        compiler_params=pltpu.CompilerParams(
            collective_id=0, has_side_effects=True, vmem_limit_bytes=22 * 2**20),
        name="exchange",
    )(*(
        pltpu.with_memory_space_constraint(a, pltpu.HBM)
        for a in (train_down, router_weight.T, router_gain.reshape(1, part))))
    flat = ready.reshape(experts * full, depth)
    pieces = 8
    out, serve = pl.pallas_call(
        functools.partial(write_kernel, pieces),
        out_shape=(
            jax.ShapeDtypeStruct((experts * full, depth), jnp.bfloat16),
            jax.ShapeDtypeStruct((owners * local, rows * part), jnp.bfloat16),
        ),
        in_specs=[vmem, vmem],
        out_specs=(anywhere, vmem),
        scratch_shapes=[pltpu.SemaphoreType.DMA((pieces,))],
        compiler_params=pltpu.CompilerParams(vmem_limit_bytes=4 * 2**20),
        name="write",
    )(flat, router)
    return out.reshape(experts, full, depth), serve.T


def solution(mesh):
    owners, rows = mesh.shape["owner"], mesh.shape["rows"]
    return jax.shard_map(
        functools.partial(on_device, owners, rows),
        mesh=mesh,
        in_specs=(P("owner", None, "rows"), P("rows", "owner"), P("rows")),
        out_specs=(P("owner", None, None), P()),
        check_vma=False,
    )
```

time: 29.5 us -> 24.1 us (0.82)
  Pallas kernels: 26.4 us -> 23.2 us
  local copies, waits for them, and re-layouts: 2.16 us -> 0 us
    pallas_call x1, Pallas kernels: 20.5 us -> 16.5 us  [on_device(): pl.pallas_call(functools.partial(exchange_kernel, owners, rows, tile), ou...]
    unnamed x4 -> x0, local copies, waits for them, and re-layouts: 1.4 us -> none
    reshape x1 -> x0, local copies, waits for them, and re-layouts: 0.77 us -> none  [on_device(): serve = router.reshape(owners * local, rows * part).T]
    pallas_call x1, Pallas kernels: 5.92 us -> 6.63 us  [on_device(): pl.pallas_call(functools.partial(write_kernel, pieces), out_shape=(jax.Sh...]
where the time goes in v2:
time: 24.1 us; the launch traced here: 23.8 us
  Pallas kernels  23.2 us (96%)
  between operations  0.64 us (3%)
    pallas_call x1, Pallas kernels, on_device(): pl.pallas_call(functools.partial(exchange_kernel, owners, rows, tile), ou...  16.5 us
    pallas_call x1, Pallas kernels, on_device(): pl.pallas_call(functools.partial(write_kernel, pieces), out_shape=(jax.Sh...  6.63 us

profile of v2, /device:TPU:0, one launch (start us, length us, event | category | flops | bytes accessed | tf_op | source)
XLA Modules:
  0.0 23.8 jit_solution(9834766030416068161)
XLA Ops:
  0.6 16.5 %exchange.1 = (bf16[4,2048,1024]{2,1,0:T(8,128)(2,1)S(1)}, bf16[16,4,2048]{2,1,0:T(4,128)(2,1)S(1)}) custom-call(f32[4,1024,1024]{2,1,0:T(8,128)} %down.1, f32[4,1024]{1,0:T(4,128)} %bitcast.6, f32[1,1024]{1,0:T(1,128)} %bitcast.7), custom_call_target="tpu_custom_call" | custom-call | tf_op jit(solution)/shard_map/exchange/pallas_call | solution.py:178
  17.2 6.6 %write.1 = (bf16[8192,1024]{1,0:T(8,128)(2,1)}, bf16[64,2048]{1,0:T(8,128)(2,1)}) custom-call(bf16[8192,1024]{1,0:T(8,128)(2,1)S(1)} %bitcast.5, bf16[16,4,2048]{2,1,0:T(4,128)(2,1)S(1)} %get-tuple-element.7.router), custom_call_target="tpu_custom_call" | custom-call | tf_op jit(solution)/shard_map/write/pallas_call | solution.py:210

commit v3 on v2

--- a/solution.py
+++ b/solution.py
@@ -9,19 +9,21 @@
 
 MESH = pl.DeviceIdType.MESH
 AHEAD = 6
+LATE = 8
 
 
 def exchange_kernel(
-    owners, rows, tile,
-    down, weight, gain, ready, router,
+    owners, rows, tile, late,
+    down, weight, gain, ready, router, later,
     landed, weight_here, gain_here, load_sem, small_sem, send_sem, recv_sem,
-    row_send, row_recv, own_send, own_recv, near, go, all_in,
+    row_send, row_recv, own_send, own_recv, near, go, all_in, later_sem,
 ):
     owner, row = lax.axis_index("owner"), lax.axis_index("rows")
     experts, _, width = down.shape
     part = weight.shape[1]
     per = width // tile
     steps = experts * per
+    early = steps - late
 
     def load(i):
         source = down.at[i // per, :, pl.ds(pl.multiple_of((i % per) * tile, tile), tile)]
@@ -107,6 +109,11 @@
         for j in range(1, rows):
             send(i, j).start()
 
+    def keep(i):
+        start = pl.multiple_of((i - early) * tile, tile)
+        return pltpu.make_async_copy(
+            place(i), later.at[pl.ds(start, tile), :], later_sem.at[i - early])
+
     turn(0)
 
     @pl.when(row != 0)
@@ -117,7 +124,7 @@
         row_copy(j).start()
         send(0, j).start()
 
-    half = max(1, steps // 2)
+    half = max(1, early // 2)
     if half > 1:
         pl.loop(1, half)(turn_and_send)
 
@@ -138,10 +145,19 @@
     def _(j):
         own_copy(j).start()
 
-    if steps > half:
-        pl.loop(half, steps)(turn_and_send)
-
-    @pl.loop(0, steps)
+    if early > half:
+        pl.loop(half, early)(turn_and_send)
+
+    @pl.loop(early, steps)
+    def _(i):
+        turn(i)
+        keep(i).start()
+
+    @pl.loop(early, steps)
+    def _(i):
+        keep(i).wait()
+
+    @pl.loop(0, early)
     def _(i):
         for j in range(1, rows):
             send(i, j).wait()
@@ -151,38 +167,79 @@
         own_copy(j).wait()
 
 
-def write_kernel(pieces, ready, router, out, serve, sems):
-    size = ready.shape[0] // pieces
+def write_kernel(rows, width, held, ready, router, out, serve, laid, sems, last_sem, serve_sem):
+    row = lax.axis_index("rows")
+    experts, full, _ = ready.shape
     local = router.shape[1]
-
-    def copy(i):
-        span = pl.ds(i * size, size)
-        return pltpu.make_async_copy(ready.at[span], out.at[span], sems.at[i])
-
-    for i in range(pieces):
-        copy(i).start()
+    whole = experts - 1
+
+    def copy(e):
+        return pltpu.make_async_copy(ready.at[e], out.at[e], sems.at[e])
+
+    def last(j):
+        start = pl.multiple_of(lax.rem(row + j, rows) * width, width)
+        span = pl.ds(start, width if j == 0 else width - held)
+        return pltpu.make_async_copy(
+            ready.at[whole, span, :], out.at[whole, span, :], last_sem.at[j])
+
+    lasts = [last(j) for j in range(rows) if j == 0 or held < width]
+    for e in range(whole):
+        copy(e).start()
+    for part in lasts:
+        part.start()
     for o in range(router.shape[0]):
-        serve[o * local:(o + 1) * local, :] = router[o]
-    for i in range(pieces):
-        copy(i).wait()
+        laid[o * local:(o + 1) * local, :] = router[o]
+    spread = pltpu.make_async_copy(laid, serve, serve_sem)
+    spread.start()
+    for e in range(whole):
+        copy(e).wait()
+    for part in lasts:
+        part.wait()
+    spread.wait()
+
+
+def put_kernel(rows, width, *refs):
+    row = lax.axis_index("rows")
+    gots, out, sems = refs[:rows - 1], refs[-2], refs[-1]
+    pieces = sems.shape[1]
+    held = gots[0].shape[0]
+    size = held // pieces
+
+    def copy(j, i):
+        source = lax.rem(row + rows - j, rows)
+        start = pl.multiple_of(source * width + (width - held) + i * size, size)
+        return pltpu.make_async_copy(
+            gots[j - 1].at[pl.ds(i * size, size), :],
+            out.at[out.shape[0] - 1, pl.ds(start, size), :], sems.at[j - 1, i])
+
+    for j in range(1, rows):
+        for i in range(pieces):
+            copy(j, i).start()
+    for j in range(1, rows):
+        for i in range(pieces):
+            copy(j, i).wait()
 
 
 def on_device(owners, rows, train_down, router_weight, router_gain):
     experts, depth, width = train_down.shape
     part, local = router_weight.shape
-    tile = min(256, width)
-    steps = experts * (width // tile)
+    tile = min(128, width)
+    per = width // tile
+    steps = experts * per
+    late = LATE if steps > LATE and per >= LATE else 1
+    held = late * tile
     vmem = pl.BlockSpec(memory_space=pltpu.VMEM)
     anywhere = pl.BlockSpec(memory_space=pl.ANY)
     full = rows * width
-    ready, router = pl.pallas_call(
-        functools.partial(exchange_kernel, owners, rows, tile),
+    ready, router, later = pl.pallas_call(
+        functools.partial(exchange_kernel, owners, rows, tile, late),
         out_shape=(
             pltpu.VMEM((experts, full, depth), jnp.bfloat16),
             pltpu.VMEM((owners, local, rows * part), jnp.bfloat16),
+            pltpu.HBM((held, depth), jnp.bfloat16),
         ),
         in_specs=[anywhere, anywhere, anywhere],
-        out_specs=(vmem, vmem),
+        out_specs=(vmem, vmem, anywhere),
         scratch_shapes=[
             pltpu.VMEM((steps, depth, tile), jnp.float32),
             pltpu.VMEM((local, part), jnp.float32),
@@ -198,6 +255,7 @@
             pltpu.SemaphoreType.REGULAR,
             pltpu.SemaphoreType.REGULAR,
             pltpu.SemaphoreType.REGULAR,
+            pltpu.SemaphoreType.DMA((late,)),
         ],
         compiler_params=pltpu.CompilerParams(
             collective_id=0, has_side_effects=True, vmem_limit_bytes=22 * 2**20),
@@ -205,21 +263,42 @@
     )(*(
         pltpu.with_memory_space_constraint(a, pltpu.HBM)
         for a in (train_down, router_weight.T, router_gain.reshape(1, part))))
-    flat = ready.reshape(experts * full, depth)
-    pieces = 8
+    got = [
+        lax.ppermute(later, "rows", [(r, (r + j) % rows) for r in range(rows)])
+        for j in range(1, rows)
+    ]
+    shape = jax.ShapeDtypeStruct((experts, full, depth), jnp.bfloat16)
     out, serve = pl.pallas_call(
-        functools.partial(write_kernel, pieces),
+        functools.partial(write_kernel, rows, width, held),
         out_shape=(
-            jax.ShapeDtypeStruct((experts * full, depth), jnp.bfloat16),
+            shape,
             jax.ShapeDtypeStruct((owners * local, rows * part), jnp.bfloat16),
         ),
         in_specs=[vmem, vmem],
-        out_specs=(anywhere, vmem),
-        scratch_shapes=[pltpu.SemaphoreType.DMA((pieces,))],
+        out_specs=(anywhere, anywhere),
+        scratch_shapes=[
+            pltpu.VMEM((owners * local, rows * part), jnp.bfloat16),
+            pltpu.SemaphoreType.DMA((experts,)),
+            pltpu.SemaphoreType.DMA((rows,)),
+            pltpu.SemaphoreType.DMA,
+        ],
         compiler_params=pltpu.CompilerParams(vmem_limit_bytes=4 * 2**20),
+        cost_estimate=pl.CostEstimate(
+            flops=0, bytes_accessed=experts * full * depth * 4, transcendentals=0),
         name="write",
-    )(flat, router)
-    return out.reshape(experts, full, depth), serve.T
+    )(ready, router)
+    pieces = 2
+    out = pl.pallas_call(
+        functools.partial(put_kernel, rows, width),
+        out_shape=shape,
+        in_specs=[vmem] * (rows - 1) + [anywhere],
+        out_specs=anywhere,
+        input_output_aliases={rows - 1: 0},
+        scratch_shapes=[pltpu.SemaphoreType.DMA((rows - 1, pieces))],
+        compiler_params=pltpu.CompilerParams(vmem_limit_bytes=2 * 2**20),
+        name="put",
+    )(*got, out)
+    return out, serve.T
 
 
 def solution(mesh):

time: 24.1 us -> 22.9 us (0.950)
  the two profiles are of different devices: /device:TPU:0 before, /device:TPU:9 now
where the time goes in v3:
time: 22.9 us; the launch traced here: 22.7 us
  Pallas kernels  20.9 us (91%)
  starting transfers between devices  1.22 us (5%)
  between operations  0.65 us (3%)
    pallas_call x1, Pallas kernels, on_device(): pl.pallas_call(functools.partial(exchange_kernel, owners, rows, tile, lat...  14.2 us
    pallas_call x1, Pallas kernels, on_device(): pl.pallas_call(functools.partial(write_kernel, rows, width, held), out_sh...  5.3 us
    pallas_call x1, Pallas kernels, on_device(): pl.pallas_call(functools.partial(put_kernel, rows, width), out_shape=shap...  1.35 us
    ppermute x1, starting transfers between devices, on_device(): lax.ppermute(later, 'rows', [(r, (r + j) % rows) for r in range(rows)])  1.22 us
  transfers between devices with their start and end apart: 1, of which 0 were waited for; matrix products, arithmetic and copies ran while one was open for 0% of the time, Pallas kernels for 23%

profile of v3, /device:TPU:9, one launch (start us, length us, event | category | flops | bytes accessed | tf_op | source)
XLA Modules:
  0.0 22.7 jit_solution(10264523843127676992)
XLA Ops:
  0.6 14.2 %exchange.1 = (bf16[4,2048,1024]{2,1,0:T(8,128)(2,1)S(1)}, bf16[16,4,2048]{2,1,0:T(4,128)(2,1)S(1)}, bf16[1024,1024]{1,0:T(8,128)(2,1)}) custom-call(f32[4,1024,1024]{2,1,0:T(8,128)} %down.1, f32[4,1024]{1,0:T(4,128)} %bitcast.3, f32[1,1024]{1,0:T(1,128)} %bitcast.4), custom_call_target="tpu_custom_call" | custom-call | tf_op jit(solution)/shard_map/exchange/pallas_call | solution.py:234
  14.9 1.2 %collective-permute-start = (bf16[1024,1024]{1,0:T(8,128)(2,1)}, bf16[1024,1024]{1,0:T(8,128)(2,1)S(1)}, u32[]{:S(2)}, u32[]{:S(2)}) collective-permute-start(bf16[1024,1024]{1,0:T(8,128)(2,1)} %get-tuple-element.7), channel_id=1, source_target_pairs={{0,1},{1,0},{2,3},{3,2},{4,5},{5,4},{6,7},{7,6},{8,9},{9,8},{10,11... | collective-permute-start | bytes 6291464 | tf_op jit(solution)/shard_map/ppermute | solution.py:267
  16.1 5.3 %write.1 = (bf16[4,2048,1024]{2,1,0:T(8,128)(2,1)}, bf16[64,2048]{1,0:T(8,128)(2,1)}) custom-call(bf16[4,2048,1024]{2,1,0:T(8,128)(2,1)S(1)} %get-tuple-element.8.ready, bf16[16,4,2048]{2,1,0:T(4,128)(2,1)S(1)} %get-tuple-element.9.router), custom_call_target="tpu_custom_call" | custom-call | bytes 33554432 | tf_op jit(solution)/shard_map/write/pallas_call | solution.py:271
  21.4 0.0 collective-permute-done.refs_0_
  21.4 1.3 %put.1 = bf16[4,2048,1024]{2,1,0:T(8,128)(2,1)} custom-call(bf16[1024,1024]{1,0:T(8,128)(2,1)S(1)} %collective-permute-done.refs_0_, bf16[4,2048,1024]{2,1,0:T(8,128)(2,1)} %get-tuple-element.10.refs_1_), custom_call_target="tpu_custom_call", output_to_operand_aliasing={{}: (1, {})} | custom-call | tf_op jit(solution)/shard_map/put/pallas_call | solution.py:291
Async XLA Ops:
  14.9 6.5 %collective-permute-start = (bf16[1024,1024]{1,0:T(8,128)(2,1)}, bf16[1024,1024]{1,0:T(8,128)(2,1)S(1)}, u32[]{:S(2)}, u32[]{:S(2)}) collective-permute-start(bf16[1024,1024]{1,0:T(8,128)(2,1)} %get-tuple-element.7), channel_id=1, source_target_pairs={{0,1},{1,0},{2,3},{3,2},{4,5},{5,4},{6,7},{7,6},{8,9},{9,8},{10,11... | collective-permute-start | bytes 6291464 | tf_op jit(solution)/shard_map/ppermute | solution.py:267
